TPU v7x, 128 devices: a whole 4x4x4 slice. The times are simulated.
128 devices in a mesh: seq: 16 (over y_hi, z, core), tp: 8 (over x, y_lo).
Axes of the slice: x: 4, y: 4 (y_hi: 2, y_lo: 2; y = y_hi * 2 + y_lo), z: 4, core: 2. Of those that a mesh axis runs over, the one named last changes fastest.
Arguments:
- streams: bfloat16 [8192, 4, 4096], P('seq', None, 'tp'), may hold values from -6 to 6
- doc_ids: int32 [8192], P('seq'), may hold values from 0 to 3, never falling along the last dimension, each value on 1 to 4096 neighbouring positions
- mix_weight: float32 [4, 4096, 24], P(None, 'tp'), may hold values from -0.046875 to 0.046875
- mix_bias: float32 [24], replicated, may hold values from -1 to 1
- attn_gain: float32 [4096], replicated, may hold values from 0.1 to 1.9
- w_qkv: bfloat16 [4096, 3, 4096], P(None, None, 'tp'), may hold values from -1 to 1
- w_out: bfloat16 [4096, 4096], P('tp'), may hold values from -0.5 to 0.5
Outputs:
- new_streams: bfloat16 [8192, 4, 4096], P('seq', None, 'tp')
Inputs may be any that keep to these rules, and one draw needn't show every extreme that they name: doc_ids never fall along the sequence; each of the 4 documents has 1 to 4096 positions, and the longest has exactly 4096.
All inputs are finite; a program needn't handle non-finite values.
Results may differ from a plain program's by a relative error of at most 0.014.
The roundings to bfloat16 on the way count: a program that leaves them out, or rounds other values in their place, can miss the bound.
Values may be sent and summed in bfloat16 or wider, within the bound.
A program may use at most 256 MiB of HBM per device.

v0:
```python
import jax
import jax.numpy as jnp
from jax import lax
from jax.sharding import Mesh
from jax.sharding import PartitionSpec as P

D = 4096
HEAD_DIM = 128
STREAMS = 4
BALANCE_ROUNDS = 20
TP = ("tp_0", "tp_1")
masked_score = -1e30
norm_eps = 1e-06


def from_everyone(x, axis):
    copies = jnp.broadcast_to(x, (lax.axis_size(axis), *x.shape))
    return lax.all_to_all(copies, axis, split_axis=0, concat_axis=0, tiled=True)


def taken_together(x, axis):
    return from_everyone(x, axis).sum(axis=0)


def packed_total(arrays, axis):
    vector, at, done = (jnp.concatenate([a.reshape(-1) for a in arrays]), 0, [])
    subtotal = taken_together(vector, axis)
    for a in arrays:
        done.append(subtotal[at : at + a.size].reshape(a.shape))
        at += a.size
    return tuple(done)


def gathered_by_axis(x, axes, dim):
    if not axes:
        return x
    nearer = lax.all_gather(x, axes[-1], axis=dim, tiled=True)
    return gathered_by_axis(nearer, axes[:-1], dim)


def summed_rows(terms, axes):
    subtotal = terms.astype(jnp.bfloat16)
    for axis in axes:
        subtotal = lax.psum_scatter(subtotal, axis, scatter_dimension=0, tiled=True)
    return subtotal.astype(jnp.float32)


def doubly_stochastic(mixing_matrix):

    def balance_round(round_index, running_matrix):
        running_matrix = running_matrix / jnp.sum(running_matrix, axis=2, keepdims=True)
        return running_matrix / jnp.sum(running_matrix, axis=1, keepdims=True)

    return lax.fori_loop(0, BALANCE_ROUNDS, balance_round, mixing_matrix)


def coefficients(squares, partial_logits, mix_bias):
    root_mean = jnp.sqrt(squares / (STREAMS * D) + norm_eps)
    coef_logits = partial_logits / root_mean[:, None] + mix_bias
    input_weights = jax.nn.sigmoid(coef_logits[:, :STREAMS])
    output_weights = 2.0 * jax.nn.sigmoid(coef_logits[:, STREAMS : 2 * STREAMS])
    unnormalized_mixing = jnp.exp(coef_logits[:, 2 * STREAMS :]).reshape(-1, STREAMS, STREAMS)
    return (input_weights, output_weights, doubly_stochastic(unnormalized_mixing))


def attend(running, queries, keys_values, key_doc, query_pos, query_doc):
    top_score, denominator, weighted = running
    key_count = keys_values.shape[0]
    heads_local = queries.shape[1]
    keys = keys_values[:, 0].reshape(key_count, heads_local, HEAD_DIM)
    values = keys_values[:, 1].reshape(key_count, heads_local, HEAD_DIM)
    scores = jnp.einsum(
        "qhd,khd->qhk", queries, keys, preferred_element_type=jnp.float32
    ) * HEAD_DIM ** (-0.5)
    key_pos = jnp.arange(key_count, dtype=jnp.int32)
    allowed = ((key_pos[None, :] <= query_pos[:, None]) & (key_doc[None, :] == query_doc[:, None]))[
        :, None, :
    ]
    scores = jnp.where(allowed, scores, masked_score)
    new_top = jnp.maximum(top_score, jnp.max(scores, axis=2))
    weights = jnp.where(allowed, jnp.exp(scores - new_top[:, :, None]), 0.0)
    denominator = jnp.sum(weights, axis=2)
    weighted = jnp.einsum(
        "qhk,khd->qhd", weights.astype(jnp.bfloat16), values, preferred_element_type=jnp.float32
    )
    return (new_top, denominator, weighted)


def local(streams, doc_ids, mix_weight, mix_bias, attn_gain, w_qkv, w_out):
    token_rows = streams.shape[0]
    width_local = streams.shape[2]
    heads_local = width_local // HEAD_DIM
    wide_streams = streams.astype(jnp.float32)
    squares = jnp.sum(wide_streams * wide_streams, axis=(1, 2))
    partial_logits = jnp.einsum(
        "tsd,sdc->tc", wide_streams, mix_weight, precision=lax.Precision.HIGHEST
    )
    squares_all, logits_all = packed_total((squares, partial_logits), TP)
    input_weights, output_weights, mixing = coefficients(squares_all, logits_all, mix_bias)
    mixed_input = jnp.einsum(
        "ts,tsd->td", input_weights, wide_streams, precision=lax.Precision.HIGHEST
    ).astype(jnp.bfloat16)
    flat_weight = w_qkv.reshape(w_qkv.shape[0], 3 * width_local)
    piece_wide = gathered_by_axis(mixed_input, TP, 1).astype(jnp.float32)
    gained = (piece_wide * attn_gain).astype(jnp.bfloat16)
    summed = jnp.dot(gained, flat_weight, preferred_element_type=jnp.float32)
    summed, square_sum = (summed, jnp.sum(piece_wide * piece_wide, axis=1))
    norm_scale = lax.rsqrt(square_sum / D + norm_eps)
    projected = (
        (summed * norm_scale[:, None]).astype(jnp.bfloat16).reshape(token_rows, 3, width_local)
    )
    queries = projected[:, 0].reshape(token_rows, heads_local, HEAD_DIM)
    keys_values = projected[:, 1:3]
    seq_index = lax.axis_index("seq")
    query_pos = seq_index * token_rows + jnp.arange(token_rows, dtype=jnp.int32)
    first_doc = doc_ids[0]
    running = (
        jnp.full((token_rows, heads_local), masked_score, jnp.float32),
        jnp.zeros((token_rows, heads_local), jnp.float32),
        jnp.zeros((token_rows, heads_local, HEAD_DIM), jnp.float32),
    )
    piece_kv = lax.all_gather(keys_values, "seq", axis=0, tiled=True)
    piece_doc = lax.all_gather(doc_ids, "seq", axis=0, tiled=True)
    needed = (jnp.int32(0) < (seq_index + 1) * token_rows) & (piece_doc[-1] >= first_doc)
    running = lax.cond(
        needed,
        lambda running_matrix: attend(
            running_matrix, queries, piece_kv, piece_doc, query_pos, doc_ids
        ),
        lambda running_matrix: running_matrix,
        running,
    )
    top_score, denominator, weighted = running
    context = (
        (weighted / denominator[:, :, None]).astype(jnp.bfloat16).reshape(token_rows, width_local)
    )
    branch_out = summed_rows(
        lax.dot_general(
            w_out, context, (((0,), (1,)), ((), ())), preferred_element_type=jnp.float32
        ),
        TP,
    )
    carried = jnp.einsum("tij,tjd->tid", mixing, wide_streams, precision=lax.Precision.HIGHEST)
    return (carried + output_weights[:, :, None] * branch_out.T[:, None, :]).astype(jnp.bfloat16)


def solution(mesh):
    split = Mesh(mesh.devices.reshape(mesh.shape["seq"], 4, 2), ("seq", "tp_0", "tp_1"))
    in_specs = (
        P("seq", None, TP),
        P("seq"),
        P(None, TP, None),
        P(),
        P(),
        P(None, None, TP),
        P(TP, None),
    )
    out_specs = P("seq", None, TP)
    return jax.shard_map(local, mesh=split, in_specs=in_specs, out_specs=out_specs, check_vma=False)
```

profile of v0, /device:TPU:1, one launch (start us, length us, event | category | flops | bytes accessed | tf_op | source)
XLA Modules:
  0.0 440.1 jit_solution(9482599936923689184)
XLA Ops:
  6.5 0.0 copy-start
  6.5 0.0 all-gather.5.cloned.1.call-start
  6.5 3.3 multiply_reduce_fusion
  9.9 0.0 copy-done
  9.9 3.6 fusion.27
  13.5 0.2 reshape.80
  13.7 0.2 broadcast_in_dim.37
  13.9 13.1 %all_to_all.6 = f32[8,1,12800]{2,1,0:T(1,128)S(1)} all-to-all(f32[8,1,12800]{2,1,0:T(1,128)S(1)} %broadcast_in_dim.37), channel_id=1, replica_groups=mesh['seq'=16,'tp_0'=4,'tp_1'=2] {'tp_0','tp_1'}, dimensions={0} | all-to-all | bytes 819200 | tf_op jit(solution)/shard_map/all_to_all | solution.py:18
  27.0 0.3 reduce_sum.55
  27.3 0.2 reshape.81
  27.5 0.1 copy.78
  27.6 0.7 divide_add_fusion
  28.4 0.1 copy.89
  28.5 5.3 %fusion.41 = bf16[512,1,512]{2,1,0:T(2,128)(2,1)S(1)} fusion(f32[512,4,1]{1,2,0:T(1,128)S(1)} %copy.89, bf16[512,4,512]{2,1,0:T(4,128)(2,1)} %param.11), kind=kOutput, calls=%fused_computation.53 | convolution fusion | flops 12582912 | bytes 2629632 | tf_op jit(solution)/shard_map/ts,tsd->td/dot_general | solution.py:100
  33.8 0.9 copy.102
  34.7 0.0 all-gather.5.cloned.1.call-update
  34.7 0.0 all-gather.7.cloned.1.call-start
  34.8 25.8 %all-gather.5.cloned.1.call-done = bf16[512,1024]{1,0:T(8,128)(2,1)} async-done(((bf16[512,512]{1,0:T(8,128)(2,1)}), bf16[512,1024]{1,0:T(8,128)(2,1)}) %all-gather.5.cloned.1.call-update) | async-done | bytes 1048592 | tf_op jit(solution)/shard_map/all_gather | solution.py:37
  60.6 0.0 all-gather.7.cloned.1.call-update
  60.6 0.0 copy-start.5
  60.6 0.2 all-gather.9.cloned.1.call-start
  60.8 17.1 %copy.81 = bf16[4096,3,512]{0,2,1:T(8,128)(2,1)} copy(bf16[4096,3,512]{2,0,1:T(8,128)(2,1)} %param.16) | data formatting | bytes 25165824 | tf_op args[5]
  78.0 33.4 %all-gather.7.cloned.1.call-done = bf16[512,4096]{1,0:T(8,128)(2,1)} async-done(((bf16[512,1024]{1,0:T(8,128)(2,1)}), bf16[512,4096]{1,0:T(8,128)(2,1)}) %all-gather.7.cloned.1.call-update) | async-done | bytes 4194320 | tf_op jit(solution)/shard_map/all_gather | solution.py:37
  111.4 3.1 fusion.14
  114.5 0.0 copy-done.5
  114.5 0.0 copy-start.4
  114.5 11.0 %fusion.22 = bf16[512,1536]{1,0:T(8,128)(2,1)S(1)} fusion(bf16[4096,1536]{0,1:T(8,128)(2,1)} %bitcast.48, bf16[512,4096]{1,0:T(8,128)(2,1)} %all-gather.7.cloned.1.call-done, f32[4096]{0:T(1024)S(1)} %copy-done.5, f32[512]{0:T(512)S(1)} %add_rsqrt_fusion), kind=kOutput, calls=%fused_computation.28 | convolution fusion | flops 6450315264 | bytes 18368512 | tf_op jit(solution)/shard_map/dot_general | solution.py:106
  125.5 0.7 copy.82
  126.2 1.0 slice.48
  127.2 0.0 all-gather.9.cloned.1.call-update
  127.3 0.0 reduce-scatter.3.cloned.1.call-start
  127.3 0.0 copy-done.4
  127.3 0.5 slice.39
  127.9 25.4 %all-gather = s32[16,1,512]{2,1,0:T(1,128)S(1)} all-gather(s32[1,1,512]{2,1,0:T(1,128)S(1)} %bitcast.58), channel_id=1, replica_groups=mesh['seq'=16,'tp_0'=4,'tp_1'=2] {'seq'}, dimensions={0}, use_global_device_ids=true | all-gather | bytes 34816 | tf_op jit(solution)/shard_map/all_gather | solution.py:123
  153.3 0.6 slice.46
  155.1 91.7 %all-gather.9.cloned.1.call-done = bf16[8192,2,512]{0,2,1:T(8,128)(2,1)} async-done(((bf16[512,2,512]{0,2,1:T(8,128)(2,1)}), bf16[8192,2,512]{0,2,1:T(8,128)(2,1)}) %all-gather.9.cloned.1.call-update) | async-done | bytes 16777232 | tf_op jit(solution)/shard_map/all_gather | solution.py:122
  246.8 103.6 %conditional.1 = (f32[512,4]{0,1:T(4,128)S(1)}, f32[512,4,128]{0,2,1:T(8,128)S(1)}) conditional(s32[]{:T(128)} %convert_element_type.35, () %tuple.18, (s32[]{:T(128)}, s32[512]{0:T(512)S(1)}, s32[8192]{0:T(1024)S(1)}, s32[512]{0:T(512)S(1)}, bf16[8192,2,512]{0,2,1:T(8,128)(2,1)}, /*index=5*/bf16[512,3,512]{0,2,1:T(8,128)(2,1)S(1)}) %tuple.51), branch_computations={%region_7.0_spmd, %region_8.11_spmd} | conditional | flops 8820619264 | bytes 290021440 | solution.py:125
  246.8 4.4 %fusion.6 = pred[512,8192]{0,1:T(8,128)(4,1)S(1)} fusion(s32[512]{0:T(512)S(1)} %get-tuple-element.37, s32[512]{0:T(512)S(1)} %broadcast_add_fusion, s32[8192]{0:T(1024)S(1)} %get-tuple-element.36), kind=kLoop, calls=%fused_computation.10 | loop fusion | flops 12582912 | bytes 4231168 | tf_op jit(solution)/shard_map/cond/branch_1_fun/and | solution.py:76
  251.2 0.0 copy-start.2
  251.2 13.1 %fusion.40 = (bf16[8192,1,512]{0,2,1:T(8,128)(2,1)}, bf16[8192,1,512]{0,2,1:T(8,128)(2,1)}) fusion(bf16[8192,2,512]{0,2,1:T(8,128)(2,1)} %get-tuple-element.38), kind=kLoop, calls=%fused_computation.52 | loop fusion | bytes 33554432 | tf_op jit(solution)/shard_map/cond/branch_1_fun/slice | solution.py:71
  264.4 0.0 copy-done.2
  264.4 27.6 %fusion = (f32[512,4]{0,1:T(4,128)S(1)}, f32[4,8192,512]{2,1,0:T(8,128)}) fusion(pred[512,8192]{0,1:T(8,128)(4,1)S(1)} %fusion.6, bf16[8192,4,128]{0,2,1:T(8,128)(2,1)} %bitcast.50, bf16[512,4,128]{0,2,1:T(8,128)(2,1)S(1)} %bitcast.55), kind=kOutput, calls=%fused_computation.4 | convolution fusion | flops 4345296896 | bytes 80224256 | tf_op jit(solution)/shard_map/cond/branch_1_fun/qhd,khd->qhk/dot_general | solution.py:72
  292.0 35.2 %fusion.7 = f32[512,4,128]{2,0,1:T(8,128)S(1)} fusion(bf16[8192,4,128]{0,2,1:T(8,128)(2,1)} %bitcast.49, f32[4,8192,512]{2,1,0:T(8,128)} %get-tuple-element.56, f32[512,4]{0,1:T(4,128)S(1)} %broadcast_maximum_fusion, pred[512,8192]{0,1:T(8,128)(4,1)} %copy-done.2), kind=kOutput, calls=%fused_computation.11 | convolution fusion | flops 4378853376 | bytes 80748544 | tf_op jit(solution)/shard_map/cond/branch_1_fun/qhk,khd->qhd/dot_general | solution.py:83
  327.2 0.3 copy.93
  327.5 22.9 %fusion.2 = f32[512,4]{0,1:T(4,128)S(1)} fusion(f32[4,8192,512]{2,1,0:T(8,128)} %get-tuple-element.56, f32[512,4]{0,1:T(4,128)S(1)} %broadcast_maximum_fusion, pred[512,8192]{0,1:T(8,128)(4,1)} %copy-done.2), kind=kLoop, calls=%fused_computation.6 | loop fusion | flops 83884032 | bytes 71319552 | tf_op jit(solution)/shard_map/cond/branch_1_fun/reduce_sum | solution.py:82
  350.4 0.1 divide_convert_fusion
  350.6 0.0 copy-start.3
  350.6 6.6 %fusion.15 = bf16[4096,512]{0,1:T(8,128)(2,1)} fusion(bf16[512,512]{0,1:T(8,128)(2,1)S(1)} %bitcast.53, bf16[512,4096]{1,0:T(8,128)(2,1)} %param.17), kind=kOutput, calls=%fused_computation.22 | convolution fusion | flops 2149580800 | bytes 8912896 | tf_op jit(solution)/shard_map/dot_general | solution.py:138
  357.2 0.0 copy-start.1
  357.2 0.0 reduce-scatter.3.cloned.1.call-update
  357.2 0.3 reduce-scatter.5.cloned.1.call-start
  357.6 43.2 %reduce-scatter.3.cloned.1.call-done = bf16[1024,512]{0,1:T(8,128)(2,1)} async-done(((bf16[4096,512]{0,1:T(8,128)(2,1)}), bf16[1024,512]{0,1:T(8,128)(2,1)}) %reduce-scatter.3.cloned.1.call-update) | async-done | bytes 1048592 | tf_op jit(solution)/shard_map/reduce_scatter | solution.py:44
  400.7 0.0 reduce-scatter.5.cloned.1.call-update
  400.7 2.1 while.10
  402.9 0.9 copy.80
  403.7 0.4 copy.79
  404.2 21.3 %reduce-scatter.5.cloned.1.call-done = bf16[512,512]{0,1:T(8,128)(2,1)} async-done(((bf16[1024,512]{0,1:T(8,128)(2,1)}), bf16[512,512]{0,1:T(8,128)(2,1)}) %reduce-scatter.5.cloned.1.call-update) | async-done | bytes 524304 | tf_op jit(solution)/shard_map/reduce_scatter | solution.py:44
  425.5 1.2 convert_bitcast_fusion
  426.7 0.0 copy-done.3
  426.7 6.9 %add_convert_fusion = bf16[512,4,512]{2,1,0:T(4,128)(2,1)} fusion(f32[512,4,4]{2,1,0:T(4,128)S(1)} %copy.79, bf16[512,4,512]{2,1,0:T(4,128)(2,1)S(1)} %copy-done.3, f32[512,512]{1,0:T(8,128)S(1)} %convert_bitcast_fusion, f32[512,4]{1,0:T(8,128)} %copy.80), kind=kOutput, calls=%fused_computation.24 | convolution fusion | flops 53477376 | bytes 5283840 | tf_op jit(solution)/shard_map/tij,tjd->tid/dot_general | solution.py:143
  433.6 0.0 copy-done.1
  (71 shorter events, 1.8 us)
Async XLA Ops:
  6.5 3.3 copy-start
  6.5 54.0 %all-gather.5.cloned.1.call-start = ((), (), s32[]{:S(2)}) async-start(), calls=%async_computation.3 | async-start | bytes 1572864 | tf_op jit(solution)/shard_map/all_gather | solution.py:37
  34.7 76.7 %all-gather.7.cloned.1.call-start = ((), (), s32[]{:S(2)}) async-start(), calls=%async_computation.4 | async-start | bytes 5242880 | tf_op jit(solution)/shard_map/all_gather | solution.py:37
  60.6 53.9 %copy-start.5 = (f32[4096]{0:T(1024)S(1)}, f32[4096]{0:T(1024)}, u32[]{:S(2)}) copy-start(f32[4096]{0:T(1024)} %param.15) | copy-start | bytes 49156
  60.6 186.2 %all-gather.9.cloned.1.call-start = ((), (), s32[]{:S(2)}) async-start(), calls=%async_computation.5 | async-start | bytes 17825792 | tf_op jit(solution)/shard_map/all_gather | solution.py:122
  114.5 12.8 %copy-start.4 = (s32[512]{0:T(512)S(1)}, s32[512]{0:T(512)}, u32[]{:S(2)}) copy-start(s32[512]{0:T(512)} %param.12) | copy-start | bytes 6148
  127.3 273.4 %reduce-scatter.3.cloned.1.call-start = ((), (), s32[]{:S(2)}) async-start(), calls=%async_computation.6 | async-start | bytes 5242880 | tf_op jit(solution)/shard_map/reduce_scatter | solution.py:44
  251.2 13.2 %copy-start.2 = (pred[512,8192]{0,1:T(8,128)(4,1)}, pred[512,8192]{0,1:T(8,128)(4,1)S(1)}, u32[]{:S(2)}) copy-start(pred[512,8192]{0,1:T(8,128)(4,1)S(1)} %fusion.6) | copy-start | bytes 12582916 | tf_op jit(solution)/shard_map/cond
  350.6 76.1 %copy-start.3 = (bf16[512,4,512]{2,1,0:T(4,128)(2,1)S(1)}, bf16[512,4,512]{2,1,0:T(4,128)(2,1)}, u32[]{:S(2)}) copy-start(bf16[512,4,512]{2,1,0:T(4,128)(2,1)} %param.11) | copy-start | bytes 6291460
  357.2 76.3 %copy-start.1 = (f32[4,512,24]{1,2,0:T(8,128)S(1)}, f32[4,512,24]{1,2,0:T(8,128)}, u32[]{:S(2)}) copy-start(f32[4,512,24]{1,2,0:T(8,128)} %param.13) | copy-start | bytes 589828
  357.2 68.3 %reduce-scatter.5.cloned.1.call-start = ((), (), s32[]{:S(2)}) async-start(), calls=%async_computation.7 | async-start | bytes 1572864 | tf_op jit(solution)/shard_map/reduce_scatter | solution.py:44
Sparse Core Ops, SparseCore 0:
  34.9 25.6 all-gather.4
  62.2 49.1 all-gather.6
  127.4 119.3 all-gather.8
  357.4 43.2 reduce-scatter.2
  402.9 22.5 reduce-scatter.4
where the time goes:
time: 441 us; the launch traced here: 440 us
  waiting for transfers between devices  215 us (49%)
  matrix products  96.2 us (22%)
  blocking collectives  38.5 us (9%)
  other arithmetic  37.8 us (9%)
  local copies, waits for them, and re-layouts  36.6 us (8%)
  between operations  14.6 us (3%)
    all_gather x1, waiting for transfers between devices, local(): piece_kv = lax.all_gather(keys_values, 'seq', axis=0, tiled=True)  91.7 us
    reduce_scatter x2, waiting for transfers between devices, summed_rows(): subtotal = lax.psum_scatter(subtotal, axis, scatter_dimension=0, tiled=True)  64.5 us
    all_gather x2, waiting for transfers between devices, gathered_by_axis(): nearer = lax.all_gather(x, axes[-1], axis=dim, tiled=True)  59.2 us
    dot_general x1, matrix products, attend(): jnp.einsum('qhk,khd->qhd', weights.astype(jnp.bfloat16), values, preferre...  35.2 us
    dot_general x1, matrix products, attend(): jnp.einsum('qhd,khd->qhk', queries, keys, preferred_element_type=jnp.floa...  27.6 us
    all_gather x1, blocking collectives, local(): piece_doc = lax.all_gather(doc_ids, 'seq', axis=0, tiled=True)  25.4 us
    reduce_sum x1, other arithmetic, attend(): denominator = jnp.sum(weights, axis=2)  22.9 us
    unnamed x11, local copies, waits for them, and re-layouts  17.2 us
  transfers between devices with their start and end apart: 5, of which 5 were waited for; matrix products, arithmetic and copies ran while one was open for 5% of the time, Pallas kernels for 0%

commit v1 on v0

--- a/solution.py
+++ b/solution.py
@@ -119,7 +119,9 @@
         jnp.zeros((token_rows, heads_local), jnp.float32),
         jnp.zeros((token_rows, heads_local, HEAD_DIM), jnp.float32),
     )
-    piece_kv = lax.all_gather(keys_values, "seq", axis=0, tiled=True)
+    piece_kv = jnp.concatenate(
+        lax.all_to_all(jnp.stack([keys_values] * lax.axis_size("seq")), "seq", 0, 0), axis=0
+    )
     piece_doc = lax.all_gather(doc_ids, "seq", axis=0, tiled=True)
     needed = (jnp.int32(0) < (seq_index + 1) * token_rows) & (piece_doc[-1] >= first_doc)
     running = lax.cond(

time: 441 us -> 613 us (1.39)
  blocking collectives: 38.5 us -> 287 us
  waiting for transfers between devices: 215 us -> 122 us
  starting transfers between devices: 0.57 us -> 8.38 us
  local copies, waits for them, and re-layouts: 36.6 us -> 44.4 us
    all_gather x1, blocking collectives: 25.4 us -> 274 us  [local(): piece_doc = lax.all_gather(doc_ids, 'seq', axis=0, tiled=True)]
    all_gather x1 -> x0, waiting for transfers between devices: 91.7 us -> none  [local(): piece_kv = lax.all_gather(keys_values, 'seq', axis=0, tiled=True)]
    reshape x0 -> x1, local copies, waits for them, and re-layouts: none -> 9.81 us  [local(): jnp.concatenate(lax.all_to_all(jnp.stack([keys_values] * lax.axis_size('s...]
    all_to_all x0 -> x1, starting transfers between devices: none -> 7.86 us  [local(): lax.all_to_all(jnp.stack([keys_values] * lax.axis_size('seq')), 'seq', 0, 0)]
    slice x1, local copies, waits for them, and re-layouts: 13.1 us -> 6.21 us  [attend(): values = keys_values[:, 1].reshape(key_count, heads_local, HEAD_DIM)]
    unnamed x11 -> x17, local copies, waits for them, and re-layouts: 17.2 us -> 17.1 us
  transfers between devices with their start and end apart: 5 -> 5, of which waited for: 5 -> 4; matrix products, arithmetic and copies ran while one was open for 5% -> 3% of each run, Pallas kernels for 0% -> 0%
where the time goes in v1:
time: 613 us; the launch traced here: 612 us
  blocking collectives  287 us (47%)
  waiting for transfers between devices  122 us (20%)
  matrix products  96.2 us (16%)
  local copies, waits for them, and re-layouts  44.4 us (7%)
  other arithmetic  38.4 us (6%)
  between operations  14.6 us (2%)
  starting transfers between devices  8.38 us (1%)
    all_gather x1, blocking collectives, local(): piece_doc = lax.all_gather(doc_ids, 'seq', axis=0, tiled=True)  274 us
    reduce_scatter x2, waiting for transfers between devices, summed_rows(): subtotal = lax.psum_scatter(subtotal, axis, scatter_dimension=0, tiled=True)  62.7 us
    all_gather x2, waiting for transfers between devices, gathered_by_axis(): nearer = lax.all_gather(x, axes[-1], axis=dim, tiled=True)  59.3 us
    dot_general x1, matrix products, attend(): jnp.einsum('qhk,khd->qhd', weights.astype(jnp.bfloat16), values, preferre...  35.2 us
    dot_general x1, matrix products, attend(): jnp.einsum('qhd,khd->qhk', queries, keys, preferred_element_type=jnp.floa...  27.6 us
    reduce_sum x1, other arithmetic, attend(): denominator = jnp.sum(weights, axis=2)  22.9 us
    unnamed x17, local copies, waits for them, and re-layouts  17.1 us
    all_to_all x1, blocking collectives, from_everyone(): return lax.all_to_all(copies, axis, split_axis=0, concat_axis=0, tiled=True)  13.1 us
  transfers between devices with their start and end apart: 5, of which 4 were waited for; matrix products, arithmetic and copies ran while one was open for 3% of the time, Pallas kernels for 0%

profile of v1, /device:TPU:1, one launch (start us, length us, event | category | flops | bytes accessed | tf_op | source)
XLA Modules:
  0.0 612.1 jit_solution(11458160309153346532)
XLA Ops:
  6.5 0.0 copy-start
  6.5 0.0 all-gather.4.cloned.1.call-start
  6.5 3.3 multiply_reduce_fusion
  9.9 0.0 copy-done
  9.9 3.6 fusion.27
  13.5 0.2 reshape.86
  13.7 0.2 broadcast_in_dim.37
  13.9 13.1 %all_to_all.11 = f32[8,1,12800]{2,1,0:T(1,128)S(1)} all-to-all(f32[8,1,12800]{2,1,0:T(1,128)S(1)} %broadcast_in_dim.37), channel_id=1, replica_groups=mesh['seq'=16,'tp_0'=4,'tp_1'=2] {'tp_0','tp_1'}, dimensions={0} | all-to-all | bytes 819200 | tf_op jit(solution)/shard_map/all_to_all | solution.py:18
  27.0 0.3 reduce_sum.55
  27.3 0.2 reshape.87
  27.5 0.1 copy.81
  27.6 0.7 divide_add_fusion
  28.3 0.6 fusion.37
  29.0 0.1 copy.93
  29.1 5.3 fusion.41
  34.4 0.9 copy.107
  35.3 0.0 all-gather.4.cloned.1.call-update
  35.3 0.2 all-gather.6.cloned.1.call-start
  35.6 25.6 %all-gather.4.cloned.1.call-done = bf16[512,1024]{1,0:T(8,128)(2,1)} async-done(((bf16[512,512]{1,0:T(8,128)(2,1)}), bf16[512,1024]{1,0:T(8,128)(2,1)}) %all-gather.4.cloned.1.call-update) | async-done | bytes 1048592 | tf_op jit(solution)/shard_map/all_gather | solution.py:37
  61.2 0.0 all-gather.6.cloned.1.call-update
  61.2 0.0 copy-start.8
  61.2 17.1 %copy.84 = bf16[4096,3,512]{0,2,1:T(8,128)(2,1)} copy(bf16[4096,3,512]{2,0,1:T(8,128)(2,1)} %param.16) | data formatting | bytes 25165824 | tf_op args[5]
  78.3 0.0 copy-done.4
  78.3 33.7 %all-gather.6.cloned.1.call-done = bf16[512,4096]{1,0:T(8,128)(2,1)} async-done(((bf16[512,1024]{1,0:T(8,128)(2,1)}), bf16[512,4096]{1,0:T(8,128)(2,1)}) %all-gather.6.cloned.1.call-update) | async-done | bytes 4194320 | tf_op jit(solution)/shard_map/all_gather | solution.py:37
  112.0 3.1 fusion.14
  115.1 0.0 copy-done.8
  115.1 11.0 %fusion.22 = bf16[512,1536]{1,0:T(8,128)(2,1)S(1)} fusion(bf16[4096,1536]{0,1:T(8,128)(2,1)} %bitcast.51, bf16[512,4096]{1,0:T(8,128)(2,1)} %all-gather.6.cloned.1.call-done, f32[4096]{0:T(1024)S(1)} %copy-done.8, f32[512]{0:T(512)S(1)} %add_rsqrt_fusion), kind=kOutput, calls=%fused_computation.28 | convolution fusion | flops 6450315264 | bytes 18368512 | tf_op jit(solution)/shard_map/dot_general | solution.py:106
  126.1 0.7 copy.85
  126.8 0.1 slice.50
  126.9 6.0 stack.2
  132.8 7.9 %all-to-all-start.1 = ((bf16[16,512,2,512]{1,3,2,0:T(8,128)(2,1)}), bf16[16,512,2,512]{1,3,2,0:T(8,128)(2,1)}, u32[]{:S(2)}, u32[]{:S(2)}) async-start(bf16[16,512,2,512]{1,3,2,0:T(8,128)(2,1)} %stack.2), calls=%async_computation.1 | async-start | bytes 33554432 | tf_op jit(solution)/shard_map/all_to_all | solution.py:123
  140.7 0.0 reduce-scatter.3.cloned.1.call-start
  140.7 0.0 copy-done.7
  140.7 0.5 slice.39
  141.3 274.4 %all-gather = s32[16,1,512]{2,1,0:T(1,128)S(1)} all-gather(s32[1,1,512]{2,1,0:T(1,128)S(1)} %bitcast.61), channel_id=1, replica_groups=mesh['seq'=16,'tp_0'=4,'tp_1'=2] {'seq'}, dimensions={0}, use_global_device_ids=true | all-gather | bytes 34816 | tf_op jit(solution)/shard_map/all_gather | solution.py:125
  415.7 0.6 slice.48
  417.5 0.0 all-to-all-done.1
  417.5 106.6 %conditional.1 = (f32[512,4]{0,1:T(4,128)S(1)}, f32[512,4,128]{0,2,1:T(8,128)S(1)}) conditional(s32[]{:T(128)} %convert_element_type.35, () %tuple.18, (s32[]{:T(128)}, s32[512]{0:T(512)S(1)}, s32[8192]{0:T(1024)S(1)}, s32[512]{0:T(512)S(1)}, bf16[16,512,2,512]{1,3,2,0:T(8,128)(2,1)}, /*index=5*/bf16[512,3,512]{0,2,1:T(8,128)(2,1)S(1)}) %tuple.53), branch_computations={%region_7.0_spmd, %region_8.11_spmd} | conditional | flops 8820619264 | bytes 323575872 | solution.py:127
  417.6 4.4 fusion.6
  422.0 0.0 copy-start.2
  422.0 9.8 %copy.101 = bf16[16,2,64,8,512]{4,3,0,2,1:T(8,128)(2,1)S(1)} copy(bf16[16,2,64,8,512]{4,3,2,1,0:T(8,128)(2,1)} %bitcast.16) | data formatting | bytes 33554432 | tf_op jit(solution)/shard_map/reshape | solution.py:122
  431.8 6.2 %fusion.40 = (bf16[8192,1,512]{0,2,1:T(8,128)(2,1)}, bf16[8192,1,512]{0,2,1:T(8,128)(2,1)}) fusion(bf16[8192,2,512]{0,2,1:T(8,128)(2,1)S(1)} %bitcast.50), kind=kLoop, calls=%fused_computation.52 | loop fusion | bytes 33554432 | tf_op jit(solution)/shard_map/cond/branch_1_fun/slice | solution.py:71
  438.1 0.0 copy-done.2
  438.1 27.6 %fusion = (f32[512,4]{0,1:T(4,128)S(1)}, f32[4,8192,512]{2,1,0:T(8,128)}) fusion(pred[512,8192]{0,1:T(8,128)(4,1)S(1)} %fusion.6, bf16[8192,4,128]{0,2,1:T(8,128)(2,1)} %bitcast.53, bf16[512,4,128]{0,2,1:T(8,128)(2,1)S(1)} %bitcast.58), kind=kOutput, calls=%fused_computation.4 | convolution fusion | flops 4345296896 | bytes 80224256 | tf_op jit(solution)/shard_map/cond/branch_1_fun/qhd,khd->qhk/dot_general | solution.py:72
  465.7 35.2 %fusion.7 = f32[512,4,128]{2,0,1:T(8,128)S(1)} fusion(bf16[8192,4,128]{0,2,1:T(8,128)(2,1)} %bitcast.52, f32[4,8192,512]{2,1,0:T(8,128)} %get-tuple-element.81, f32[512,4]{0,1:T(4,128)S(1)} %broadcast_maximum_fusion, pred[512,8192]{0,1:T(8,128)(4,1)} %copy-done.2), kind=kOutput, calls=%fused_computation.11 | convolution fusion | flops 4378853376 | bytes 80748544 | tf_op jit(solution)/shard_map/cond/branch_1_fun/qhk,khd->qhd/dot_general | solution.py:83
  500.9 0.3 copy.97
  501.3 22.9 %fusion.2 = f32[512,4]{0,1:T(4,128)S(1)} fusion(f32[4,8192,512]{2,1,0:T(8,128)} %get-tuple-element.81, f32[512,4]{0,1:T(4,128)S(1)} %broadcast_maximum_fusion, pred[512,8192]{0,1:T(8,128)(4,1)} %copy-done.2), kind=kLoop, calls=%fused_computation.6 | loop fusion | flops 83884032 | bytes 71319552 | tf_op jit(solution)/shard_map/cond/branch_1_fun/reduce_sum | solution.py:82
  524.1 0.0 copy-start.5
  524.2 0.0 copy-start.6
  524.2 0.1 divide_convert_fusion
  524.3 0.0 copy-start.3
  524.3 6.6 %fusion.15 = bf16[4096,512]{0,1:T(8,128)(2,1)} fusion(bf16[512,512]{0,1:T(8,128)(2,1)S(1)} %bitcast.56, bf16[512,4096]{1,0:T(8,128)(2,1)} %param.17), kind=kOutput, calls=%fused_computation.22 | convolution fusion | flops 2149580800 | bytes 8912896 | tf_op jit(solution)/shard_map/dot_general | solution.py:140
  531.0 0.0 reduce-scatter.3.cloned.1.call-update
  531.0 0.3 reduce-scatter.5.cloned.1.call-start
  531.3 0.0 copy-done.5
  531.3 41.4 %reduce-scatter.3.cloned.1.call-done = bf16[1024,512]{0,1:T(8,128)(2,1)} async-done(((bf16[4096,512]{0,1:T(8,128)(2,1)}), bf16[1024,512]{0,1:T(8,128)(2,1)}) %reduce-scatter.3.cloned.1.call-update) | async-done | bytes 1048592 | tf_op jit(solution)/shard_map/reduce_scatter | solution.py:44
  572.7 0.0 reduce-scatter.5.cloned.1.call-update
  572.7 2.1 while.10
  574.9 0.0 copy-done.6
  574.9 0.8 copy.83
  575.7 0.4 copy.82
  576.2 21.3 %reduce-scatter.5.cloned.1.call-done = bf16[512,512]{0,1:T(8,128)(2,1)} async-done(((bf16[1024,512]{0,1:T(8,128)(2,1)}), bf16[512,512]{0,1:T(8,128)(2,1)}) %reduce-scatter.5.cloned.1.call-update) | async-done | bytes 524304 | tf_op jit(solution)/shard_map/reduce_scatter | solution.py:44
  597.5 1.2 convert_bitcast_fusion
  598.7 6.9 %add_convert_fusion = bf16[512,4,512]{2,1,0:T(4,128)(2,1)} fusion(f32[512,4,4]{2,1,0:T(4,128)S(1)} %copy.82, bf16[512,4,512]{2,1,0:T(4,128)(2,1)S(1)} %copy-done.3, f32[512,512]{1,0:T(8,128)S(1)} %convert_bitcast_fusion, f32[512,4]{1,0:T(8,128)} %copy.83), kind=kOutput, calls=%fused_computation.24 | convolution fusion | flops 53477376 | bytes 5283840 | tf_op jit(solution)/shard_map/tij,tjd->tid/dot_general | solution.py:145
  (75 shorter events, 1.8 us)
Async XLA Ops:
  6.5 3.3 copy-start
  6.5 54.6 %all-gather.4.cloned.1.call-start = ((), (), s32[]{:S(2)}) async-start(), calls=%async_computation.4 | async-start | bytes 1572864 | tf_op jit(solution)/shard_map/all_gather | solution.py:37
  28.3 49.9 %copy-start.4 = (f32[512,24]{0,1:T(8,128)}, f32[512,24]{0,1:T(8,128)S(1)}, u32[]{:S(2)}) copy-start(f32[512,24]{0,1:T(8,128)S(1)} %divide_add_fusion) | copy-start | bytes 147460
  35.3 76.7 %all-gather.6.cloned.1.call-start = ((), (), s32[]{:S(2)}) async-start(), calls=%async_computation.5 | async-start | bytes 5242880 | tf_op jit(solution)/shard_map/all_gather | solution.py:37
  61.2 53.9 %copy-start.8 = (f32[4096]{0:T(1024)S(1)}, f32[4096]{0:T(1024)}, u32[]{:S(2)}) copy-start(f32[4096]{0:T(1024)} %param.15) | copy-start | bytes 49156
  132.8 7.9 %copy-start.7 = (s32[512]{0:T(512)S(1)}, s32[512]{0:T(512)}, u32[]{:S(2)}) copy-start(s32[512]{0:T(512)} %param.12) | copy-start | bytes 6148
  132.8 284.7 %all-to-all-start.1 = ((bf16[16,512,2,512]{1,3,2,0:T(8,128)(2,1)}), bf16[16,512,2,512]{1,3,2,0:T(8,128)(2,1)}, u32[]{:S(2)}, u32[]{:S(2)}) async-start(bf16[16,512,2,512]{1,3,2,0:T(8,128)(2,1)} %stack.2), calls=%async_computation.1 | async-start | bytes 33554432 | tf_op jit(solution)/shard_map/all_to_all | solution.py:123
  140.7 432.0 %reduce-scatter.3.cloned.1.call-start = ((), (), s32[]{:S(2)}) async-start(), calls=%async_computation.6 | async-start | bytes 5242880 | tf_op jit(solution)/shard_map/reduce_scatter | solution.py:44
  422.0 16.1 %copy-start.2 = (pred[512,8192]{0,1:T(8,128)(4,1)}, pred[512,8192]{0,1:T(8,128)(4,1)S(1)}, u32[]{:S(2)}) copy-start(pred[512,8192]{0,1:T(8,128)(4,1)S(1)} %fusion.6) | copy-start | bytes 12582916 | tf_op jit(solution)/shard_map/cond
  524.1 7.1 %copy-start.5 = (f32[512,24]{0,1:T(8,128)S(1)}, f32[512,24]{0,1:T(8,128)}, u32[]{:S(2)}) copy-start(f32[512,24]{0,1:T(8,128)} %copy-done.4) | copy-start | bytes 147460
  524.2 50.7 %copy-start.6 = (f32[512,4]{0,1:T(4,128)S(1)}, f32[512,4]{0,1:T(4,128)}, u32[]{:S(2)}) copy-start(f32[512,4]{0,1:T(4,128)} %get-tuple-element.82) | copy-start | bytes 24580
  524.3 74.4 %copy-start.3 = (bf16[512,4,512]{2,1,0:T(4,128)(2,1)S(1)}, bf16[512,4,512]{2,1,0:T(4,128)(2,1)}, u32[]{:S(2)}) copy-start(bf16[512,4,512]{2,1,0:T(4,128)(2,1)} %param.11) | copy-start | bytes 6291460
  531.0 74.6 %copy-start.1 = (f32[4,512,24]{1,2,0:T(8,128)S(1)}, f32[4,512,24]{1,2,0:T(8,128)}, u32[]{:S(2)}) copy-start(f32[4,512,24]{1,2,0:T(8,128)} %param.13) | copy-start | bytes 589828
  531.0 66.5 %reduce-scatter.5.cloned.1.call-start = ((), (), s32[]{:S(2)}) async-start(), calls=%async_computation.7 | async-start | bytes 1572864 | tf_op jit(solution)/shard_map/reduce_scatter | solution.py:44
Sparse Core Ops, SparseCore 0:
  35.5 25.6 all-gather.3
  62.8 49.1 all-gather.5
  531.1 41.5 reduce-scatter.2
  574.9 22.5 reduce-scatter.4
